TPU v7x, 256 devices: a whole 4x4x8 slice. The times are simulated.
256 devices in a mesh: site: 64 (over z, x, core), dom: 4 (over y).
Axes of the slice: x: 4, y: 4, z: 8, core: 2. Of those that a mesh axis runs over, the one named last changes fastest.
Arguments:
- top_partial: float32 [16, 61, 4, 65536], P(None, None, 'dom', 'site'), may hold values from 0.001 to 1
- bottom_partial: float32 [16, 61, 4, 65536], P(None, None, 'dom', 'site'), may hold values from 0.001 to 1
- left_vectors: float32 [256, 61, 61], P('dom'), may hold values from 0.05 to 1
- right_vectors: float32 [256, 61, 61], P('dom'), may hold values from 0.05 to 1
- decay_rates: float32 [256, 61], P('dom'), may hold values from 0.05 to 8
- state_weights: float32 [256, 61], P('dom'), may hold values from 0.002 to 0.05
- part_rates: float32 [256], P('dom'), may hold values from 0.3 to 3
- branch_lengths: float32 [1997], replicated, may hold values from 0.02 to 0.5
- pattern_weights: int32 [4, 65536], P('dom', 'site'), may hold values from 0 to 9
- block_partition: int32 [4, 512], P('dom', 'site'), may hold values from 0 to 255
- chosen_branches: int32 [16], replicated, may hold values from 0 to 1996, as said below
Outputs:
- site_loglik: float32 [16, 4, 65536], P(None, 'dom', 'site')
- part_derivs: float32 [2, 16, 256], P(None, None, 'dom')
- new_lengths: float32 [1997], replicated
Inputs may be any that keep to these rules, and one draw needn't show every extreme that they name: `chosen_branches`: distinct branch numbers.
All inputs are finite; a program needn't handle non-finite values.
Results may differ from a plain program's by a relative error of at most 0.0003.
Values sent between devices are 32-bit elements; how exact they have to be, the bound alone decides.
A program may use at most 64 MiB of HBM per device.

v0:
```python
import math
import jax
import jax.numpy as jnp
from jax import lax
from jax.sharding import PartitionSpec as P

BLK = 128


def in_one_piece(arrays, axis, split_dim, concat_dim, along):
    widths = [math.prod(a.shape[along:]) for a in arrays]
    both = jnp.concatenate(
        [a.reshape(*a.shape[:along], w) for a, w in zip(arrays, widths)], axis=along
    )
    out = lax.all_to_all(both, axis, split_axis=split_dim, concat_axis=concat_dim, tiled=True)
    parts = jnp.split(out, [sum(widths[:k]) for k in range(1, len(widths))], axis=along)
    return tuple((b.reshape(*out.shape[:along], *a.shape[along:]) for a, b in zip(arrays, parts)))


def cut_along(x, dim, count):
    dims = x.shape
    parts = x.reshape(*dims[:dim], count, dims[dim] // count, *dims[dim + 1 :])
    return jnp.moveaxis(parts, dim, 0)


def sum_at_owner(x, axis, dim):
    count = lax.axis_size(axis)
    parts = lax.all_to_all(cut_along(x, dim, count), axis, 0, 0, tiled=True)
    return jnp.sum(parts, axis=0)


def copy_for_each(x, axis):
    count = lax.axis_size(axis)
    return lax.all_to_all(jnp.broadcast_to(x[None], (count, *x.shape)), axis, 0, 0, tiled=True)


def of_everyone(x, axis):
    return copy_for_each(x, axis).sum(axis=0)


def project(upper, lower, vec_left, vec_right, state_w):
    scaled = upper * jnp.transpose(state_w)[None, :, :, None]
    lefts = jnp.einsum("binl,nik->bknl", scaled, vec_left, precision=lax.Precision.HIGHEST)
    rights = jnp.einsum("nkj,bjnl->bknl", vec_right, lower, precision=lax.Precision.HIGHEST)
    return (lefts, rights)


def finish(lefts, rights, exponent, times, weight_f):
    joint = lefts * rights
    expo = jnp.transpose(exponent)[None, :, :, None]
    decayed = joint * jnp.exp(expo * times[:, None, None, None])
    like_zero = jnp.sum(decayed, axis=1)
    like_one = jnp.sum(decayed * expo, axis=1)
    like_two = jnp.sum(decayed * expo * expo, axis=1)
    first = like_one / like_zero
    second = like_two / like_zero - first * first
    loglik = weight_f[None] * jnp.log(like_zero)
    sums = jnp.stack(
        [jnp.sum(weight_f[None] * first, axis=-1), jnp.sum(weight_f[None] * second, axis=-1)]
    )
    return (loglik, sums)


def on_device(
    top_partial,
    bottom_partial,
    left_vectors,
    right_vectors,
    decay_rates,
    state_weights,
    part_rates,
    branch_lengths,
    pattern_weights,
    block_partition,
    chosen_branches,
):
    times = branch_lengths[chosen_branches]
    branches = top_partial.shape[0]
    states = top_partial.shape[1]
    sites_here = top_partial.shape[3]
    nblocks = sites_here // BLK
    upper = top_partial.reshape(branches, states, nblocks, BLK)
    lower = bottom_partial.reshape(branches, states, nblocks, BLK)
    blocks = block_partition[0]
    owned = left_vectors.shape[0]
    groups = lax.axis_size("dom")
    parts_all = owned * groups
    wanted = lax.all_gather(block_partition, "dom", axis=0, tiled=True)
    relative = wanted - lax.axis_index("dom") * owned
    inside = jnp.logical_and(relative >= 0, relative < owned).astype(jnp.float32)
    clipped = jnp.clip(relative, 0, owned - 1)
    send_left = left_vectors[clipped] * inside[:, :, None, None]
    send_right = right_vectors[clipped] * inside[:, :, None, None]
    send_decay = decay_rates[clipped] * inside[:, :, None]
    send_weight = state_weights[clipped] * inside[:, :, None]
    send_rate = part_rates[clipped] * inside
    received = in_one_piece(
        (send_left, send_right, send_decay, send_weight, send_rate), "dom", 0, 0, 2
    )
    vec_left = jnp.sum(received[0], axis=0)
    vec_right = jnp.sum(received[1], axis=0)
    decay_b = jnp.sum(received[2], axis=0)
    weight_b = jnp.sum(received[3], axis=0)
    rate_b = jnp.sum(received[4], axis=0)
    exponent = -decay_b * rate_b[:, None]
    lefts, rights = project(upper, lower, vec_left, vec_right, weight_b)
    weight_f = pattern_weights[0].astype(jnp.float32).reshape(nblocks, BLK)
    loglik, sums = finish(lefts, rights, exponent, times, weight_f)
    onehot = (blocks[:, None] == jnp.arange(parts_all, dtype=jnp.int32)[None, :]).astype(
        jnp.float32
    )
    part_local = jnp.einsum("abn,np->abp", sums, onehot, precision=lax.Precision.HIGHEST)
    share = sum_at_owner(part_local, "dom", 2)
    share = of_everyone(share, "site")
    totals = of_everyone(jnp.sum(share, axis=2), "dom")
    updated = times - totals[0] / totals[1]
    new_lengths = branch_lengths.at[chosen_branches].set(updated)
    return (loglik.reshape(branches, 1, sites_here), share, new_lengths)


def solution(mesh):
    return jax.shard_map(
        on_device,
        mesh=mesh,
        in_specs=(
            P(None, None, "dom", "site"),
            P(None, None, "dom", "site"),
            P("dom", None, None),
            P("dom", None, None),
            P("dom", None),
            P("dom", None),
            P("dom"),
            P(),
            P("dom", "site"),
            P("dom", "site"),
            P(),
        ),
        out_specs=(P(None, "dom", "site"), P(None, None, "dom"), P()),
        check_vma=False,
    )
```

profile of v0, /device:TPU:2, one launch (start us, length us, event | category | flops | bytes accessed | tf_op | source)
XLA Modules:
  0.0 121.1 jit_solution(9104302624612339698)
XLA Ops:
  0.6 0.0 copy-start
  0.6 0.8 copy.97
  1.5 10.1 %all-gather = s32[4,1,8]{2,1,0:T(1,128)S(1)} all-gather(s32[1,1,8]{2,1,0:T(1,128)} %bitcast.49), channel_id=1, replica_groups=mesh['site'=64,'dom'=4] {'dom'}, dimensions={0}, use_global_device_ids=true | all-gather | bytes 160 | tf_op jit(solution)/shard_map/all_gather | solution.py:88
  11.7 0.1 reshape.90
  11.7 1.4 %gather_fusion.4 = f32[32]{0:T(128)S(1)} fusion(f32[64]{0:T(128)} %param.17, s32[1024]{0:T(1024)S(1)} %pad_clamp_fusion.1), kind=kCustom, calls=%fused_computation.4 | custom fusion | bytes 384 | tf_op jit(solution)/shard_map/gather | solution.py:96
  13.1 0.1 reshape.121
  13.2 0.6 select_bitcast_fusion
  13.8 0.0 copy-done
  13.8 2.7 %gather_fusion = f32[32,61,61]{2,0,1:T(8,128)S(1)} fusion(f32[64,61,61]{2,0,1:T(8,128)S(1)} %copy-done, s32[1024]{0:T(1024)S(1)} %pad_clamp_fusion.1), kind=kCustom, calls=%fused_computation | custom fusion | bytes 952704 | tf_op jit(solution)/shard_map/gather | solution.py:92
  16.5 1.6 %copy.60 = f32[32,61,61]{2,1,0:T(8,128)} copy(f32[32,61,61]{2,0,1:T(8,128)S(1)} %gather_fusion) | data formatting | bytes 952576 | tf_op jit(solution)/shard_map/gather | solution.py:92
  18.1 1.7 %gather.23 = f32[4,8,3721]{2,1,0:T(8,128)S(1)} reshape(f32[32,61,61]{2,1,0:T(8,128)} %copy.60) | data formatting | bytes 952576 | tf_op jit(solution)/shard_map/gather | solution.py:92
  19.8 0.0 copy-start.2
  19.8 4.0 %gather_fusion.1 = f32[32,61,61]{2,0,1:T(8,128)S(1)} fusion(f32[64,61,61]{2,0,1:T(8,128)} %param.14, s32[1024]{0:T(1024)S(1)} %pad_clamp_fusion.1), kind=kCustom, calls=%fused_computation.1 | custom fusion | bytes 952704 | tf_op jit(solution)/shard_map/gather | solution.py:93
  23.9 1.6 %copy.61 = f32[32,61,61]{2,1,0:T(8,128)} copy(f32[32,61,61]{2,0,1:T(8,128)S(1)} %gather_fusion.1) | data formatting | bytes 952576 | tf_op jit(solution)/shard_map/gather | solution.py:93
  25.4 1.7 %gather.25 = f32[4,8,3721]{2,1,0:T(8,128)S(1)} reshape(f32[32,61,61]{2,1,0:T(8,128)} %copy.61) | data formatting | bytes 952576 | tf_op jit(solution)/shard_map/gather | solution.py:93
  27.2 0.0 copy-done.2
  27.2 0.6 gather_fusion.2
  27.8 1.3 %gather_fusion.3 = f32[32,61]{1,0:T(8,128)S(1)} fusion(f32[64,61]{1,0:T(8,128)} %param.16, s32[1024]{0:T(1024)S(1)} %pad_clamp_fusion.1), kind=kCustom, calls=%fused_computation.3 | custom fusion | bytes 15744 | tf_op jit(solution)/shard_map/gather | solution.py:95
  29.1 0.8 copy.62
  29.9 0.9 broadcast_multiply_fusion
  30.8 0.1 bitcast_multiply_fusion.1
  30.9 2.2 %concatenate.3 = f32[4,8,7565]{2,1,0:T(8,128)} concatenate(f32[4,8,3721]{2,1,0:T(8,128)} %get-tuple-element.29, f32[4,8,3721]{2,1,0:T(8,128)S(1)} %get-tuple-element.28, f32[4,8,61]{2,1,0:T(8,128)S(1)} %get-tuple-element.27, f32[4,8,61]{2,1,0:T(8,128)S(1)} %get-tuple-element.26, f32[4,8,1]{2,1,0:T(8,128)S(1)} %copy.62), dimensions={2} | concatenate | bytes 1936640 | tf_op jit(solution)/shard_map/concatenate | solution.py:12
  33.1 3.5 %all-to-all-start = ((f32[4,8,7565]{2,1,0:T(8,128)}), f32[4,8,7565]{2,1,0:T(8,128)S(1)}, u32[]{:S(2)}, u32[]{:S(2)}) async-start(f32[4,8,7565]{2,1,0:T(8,128)} %concatenate.3), calls=%async_computation | async-start | bytes 1966080 | tf_op jit(solution)/shard_map/all_to_all | solution.py:15
  36.6 0.7 convert_element_type.18
  37.3 0.7 compare_select_fusion.1
  37.9 0.7 gather_fusion.5
  38.6 11.0 %all-to-all-done = f32[4,8,7565]{2,1,0:T(8,128)S(1)} async-done(((f32[4,8,7565]{2,1,0:T(8,128)}), f32[4,8,7565]{2,1,0:T(8,128)S(1)}, u32[]{:S(2)}, u32[]{:S(2)}) %all-to-all-start) | async-done | bytes 968352 | tf_op jit(solution)/shard_map/all_to_all | solution.py:15
  49.6 0.2 slice_reduce_fusion.1
  49.8 0.3 reshape.171
  50.1 1.0 reduce_sum.131
  51.0 0.1 slice_reduce_fusion.4
  51.1 0.2 slice_reduce_fusion.2
  51.3 0.1 multiply_bitcast_fusion
  51.4 0.1 multiply_exponential_fusion
  51.5 0.0 copy-start.3
  51.5 0.0 copy-start.5
  51.5 6.8 %fusion = f32[8,61,16,128]{3,1,2,0:T(8,128)S(1)} fusion(f32[16,61,8,128]{3,2,1,0:T(8,128)} %bitcast.41, f32[8,61,61,1]{2,1,0,3:T(8,128)S(1)} %reshape.171), kind=kOutput, calls=%fused_computation.8 | convolution fusion | flops 731578368 | bytes 8114464 | tf_op jit(solution)/shard_map/nkj,bjnl->bknl/dot_general | solution.py:44
  58.3 0.0 copy-done.3
  58.3 0.0 copy-done.5
  58.3 0.0 copy-start.4
  58.3 6.4 %multiply_reduce_fusion.1 = (f32[16,8,128]{2,0,1:T(8,128)S(1)}, f32[16,8,128]{2,0,1:T(8,128)S(1)}, f32[16,8,128]{2,0,1:T(8,128)S(1)}) fusion(f32[61,8]{0,1:T(8,128)S(1)} %multiply_bitcast_fusion, f32[16,61,8]{1,0,2:T(8,128)S(1)} %multiply_exponential_fusion, f32[8,61,16,128]{3,1,2,0:T(8,128)S(1)} %fusion, f32[16,61,8,128]{3,2,1,0:T(8,128)S(1)} %bitcast.51, ...), kind=kOutput, calls=%fused_computation.13 | convolution fusion | flops 739524608 | bytes 8346208 | tf_op jit(solution)/shard_map/binl,nik->bknl/dot_general | solution.py:43
  64.7 0.1 multiply_reduce_fusion.3
  64.8 0.0 copy-done.4
  64.8 0.2 fusion.6
  65.1 0.1 reshape.87
  65.2 0.1 reshape.174
  65.3 7.8 %all_to_all.20 = f32[4,1,2048]{2,1,0:T(1,128)S(1)} all-to-all(f32[4,1,2048]{2,1,0:T(1,128)S(1)} %reshape.174), channel_id=1, replica_groups=mesh['site'=64,'dom'=4] {'dom'}, dimensions={0} | all-to-all | bytes 65536 | tf_op jit(solution)/shard_map/all_to_all | solution.py:28
  73.1 0.5 broadcast.90
  73.6 0.7 reduce.4
  74.3 0.1 reshape.175
  74.4 0.1 broadcast_in_dim.10
  74.6 1.4 %reshape.176 = f32[64,1,2048]{2,1,0:T(1,128)} reshape(f32[64,2,16,64]{3,2,1,0:T(8,128)S(1)} %broadcast_in_dim.10) | data formatting | bytes 1048576
  76.0 12.1 %all-to-all-start.2 = ((f32[64,1,2048]{2,1,0:T(1,128)}), f32[64,1,2048]{2,1,0:T(1,128)S(1)}, u32[]{:S(2)}, u32[]{:S(2)}) async-start(f32[64,1,2048]{2,1,0:T(1,128)} %reshape.176), calls=%async_computation.2 | async-start | bytes 1048576 | tf_op jit(solution)/shard_map/all_to_all | solution.py:34
  88.2 17.5 %all-to-all-done.2 = f32[64,1,2048]{2,1,0:T(1,128)S(1)} async-done(((f32[64,1,2048]{2,1,0:T(1,128)}), f32[64,1,2048]{2,1,0:T(1,128)S(1)}, u32[]{:S(2)}, u32[]{:S(2)}) %all-to-all-start.2) | async-done | bytes 524320 | tf_op jit(solution)/shard_map/all_to_all | solution.py:34
  105.7 2.8 %reduce.5 = f32[64,2048]{1,0:T(8,128)} reduce(f32[64,1,2048]{2,1,0:T(1,128)S(1)} %all-to-all-done.2, f32[]{:T(128)} %broadcast.90), dimensions={1}, to_apply=%all_to_all.14.reduce_sub_computation | reduce | bytes 1048580 | tf_op jit(solution)/shard_map/all_to_all | solution.py:34
  108.5 1.5 %reshape.177 = f32[64,2,16,64]{3,2,1,0:T(8,128)S(1)} reshape(f32[64,2048]{1,0:T(8,128)} %reduce.5) | data formatting | bytes 1048576
  110.0 0.7 fusion.14
  110.7 0.6 broadcast_in_dim.11
  111.3 3.2 %all-to-all-start.3 = ((f32[4,2,16]{2,1,0:T(2,128)}), f32[4,2,16]{2,1,0:T(2,128)S(1)}, u32[]{:S(2)}, u32[]{:S(2)}) async-start(f32[4,2,16]{2,1,0:T(2,128)} %broadcast_in_dim.11), calls=%async_computation.3 | async-start | bytes 8192 | tf_op jit(solution)/shard_map/all_to_all | solution.py:34
  114.5 0.7 copy.73
  115.2 4.5 %all-to-all-done.3 = f32[4,2,16]{2,1,0:T(2,128)S(1)} async-done(((f32[4,2,16]{2,1,0:T(2,128)}), f32[4,2,16]{2,1,0:T(2,128)S(1)}, u32[]{:S(2)}, u32[]{:S(2)}) %all-to-all-start.3) | async-done | bytes 544 | tf_op jit(solution)/shard_map/all_to_all | solution.py:34
  119.8 0.6 scatter_fusion
  120.5 0.0 copy-start.1
  120.5 0.6 copy-done.1
  (13 shorter events, 0.1 us)
Async XLA Ops:
  0.6 13.2 %copy-start = (f32[64,61,61]{2,0,1:T(8,128)S(1)}, f32[64,61,61]{2,0,1:T(8,128)}, u32[]{:S(2)}) copy-start(f32[64,61,61]{2,0,1:T(8,128)} %param.13) | copy-start | bytes 2857732
  19.8 7.4 %copy-start.2 = (f32[64,61]{1,0:T(8,128)S(1)}, f32[64,61]{1,0:T(8,128)}, u32[]{:S(2)}) copy-start(f32[64,61]{1,0:T(8,128)} %param.15) | copy-start | bytes 46852
  33.1 16.5 %all-to-all-start = ((f32[4,8,7565]{2,1,0:T(8,128)}), f32[4,8,7565]{2,1,0:T(8,128)S(1)}, u32[]{:S(2)}, u32[]{:S(2)}) async-start(f32[4,8,7565]{2,1,0:T(8,128)} %concatenate.3), calls=%async_computation | async-start | bytes 1966080 | tf_op jit(solution)/shard_map/all_to_all | solution.py:15
  51.5 6.8 %copy-start.3 = (f32[8,61,61]{2,1,0:T(8,128)S(1)}, f32[8,61,61]{2,1,0:T(8,128)}, u32[]{:S(2)}) copy-start(f32[8,61,61]{2,1,0:T(8,128)} %reduce_sum.131) | copy-start | bytes 357220
  51.5 6.8 %copy-start.5 = (f32[16,61,1,1024]{3,2,1,0:T(1,128)S(1)}, f32[16,61,1,1024]{3,2,1,0:T(1,128)}, u32[]{:S(2)}) copy-start(f32[16,61,1,1024]{3,2,1,0:T(1,128)} %param.11) | copy-start | bytes 11993092
  58.3 6.5 %copy-start.4 = (s32[1,8]{1,0:T(1,128)S(1)}, s32[1,8]{1,0:T(1,128)}, u32[]{:S(2)}) copy-start(s32[1,8]{1,0:T(1,128)} %param.20) | copy-start | bytes 100
  76.0 29.7 %all-to-all-start.2 = ((f32[64,1,2048]{2,1,0:T(1,128)}), f32[64,1,2048]{2,1,0:T(1,128)S(1)}, u32[]{:S(2)}, u32[]{:S(2)}) async-start(f32[64,1,2048]{2,1,0:T(1,128)} %reshape.176), calls=%async_computation.2 | async-start | bytes 1048576 | tf_op jit(solution)/shard_map/all_to_all | solution.py:34
  111.3 8.5 %all-to-all-start.3 = ((f32[4,2,16]{2,1,0:T(2,128)}), f32[4,2,16]{2,1,0:T(2,128)S(1)}, u32[]{:S(2)}, u32[]{:S(2)}) async-start(f32[4,2,16]{2,1,0:T(2,128)} %broadcast_in_dim.11), calls=%async_computation.3 | async-start | bytes 8192 | tf_op jit(solution)/shard_map/all_to_all | solution.py:34
  120.5 0.6 copy-start.1
where the time goes:
time: 122 us; the launch traced here: 121 us
  waiting for transfers between devices  33 us (27%)
  local copies, waits for them, and re-layouts  29 us (24%)
  starting transfers between devices  18.9 us (15%)
  blocking collectives  17.9 us (15%)
  matrix products  13.4 us (11%)
  other arithmetic  8 us (7%)
    all_to_all x2, waiting for transfers between devices, copy_for_each(): lax.all_to_all(jnp.broadcast_to(x[None], (count, *x.shape)), axis, 0, 0,...  22 us
    all_to_all x2, starting transfers between devices, copy_for_each(): lax.all_to_all(jnp.broadcast_to(x[None], (count, *x.shape)), axis, 0, 0,...  15.4 us
    all_to_all x1, waiting for transfers between devices, in_one_piece(): lax.all_to_all(both, axis, split_axis=split_dim, concat_axis=concat_dim,...  11 us
    all_gather x1, blocking collectives, on_device(): wanted = lax.all_gather(block_partition, 'dom', axis=0, tiled=True)  10.1 us
    all_to_all x1, blocking collectives, sum_at_owner(): parts = lax.all_to_all(cut_along(x, dim, count), axis, 0, 0, tiled=True)  7.8 us
    gather x3, local copies, waits for them, and re-layouts, on_device(): send_right = right_vectors[clipped] * inside[:, :, None, None]  7.34 us
    dot_general x1, matrix products, project(): jnp.einsum('nkj,bjnl->bknl', vec_right, lower, precision=lax.Precision.HI...  6.79 us
    dot_general x1, matrix products, project(): jnp.einsum('binl,nik->bknl', scaled, vec_left, precision=lax.Precision.HI...  6.36 us
  transfers between devices with their start and end apart: 3, of which 3 were waited for; matrix products, arithmetic and copies ran while one was open for 2% of the time, Pallas kernels for 0%

commit v1 on v0

--- a/solution.py
+++ b/solution.py
@@ -5,6 +5,12 @@
 from jax.sharding import PartitionSpec as P
 
 BLK = 128
+
+
+def laid_out(blocks, dim):
+    shape = list(blocks.shape[1:])
+    shape[dim] *= blocks.shape[0]
+    return jnp.moveaxis(blocks, 0, dim).reshape(shape)
 
 
 def in_one_piece(arrays, axis, split_dim, concat_dim, along):
@@ -85,7 +91,19 @@
     owned = left_vectors.shape[0]
     groups = lax.axis_size("dom")
     parts_all = owned * groups
-    wanted = lax.all_gather(block_partition, "dom", axis=0, tiled=True)
+    size = lax.axis_size("dom")
+    pairs = [(i, (i + 1) % size) for i in range(size)]
+    back = [(b_2, a_2) for a_2, b_2 in pairs]
+    lower_2, upper_2 = ([], [])
+    for lap in range(size - 1):
+        if lap % 2 == 0:
+            lower_2.append(lax.ppermute(lower_2[-1] if lower_2 else block_partition, "dom", pairs))
+        else:
+            upper_2.append(lax.ppermute(upper_2[-1] if upper_2 else block_partition, "dom", back))
+    blocks_2 = jnp.stack([*lower_2[::-1], block_partition, *upper_2])
+    shift = lax.axis_index("dom") - len(lower_2)
+    blocks_2 = blocks_2[(jnp.arange(size) - shift) % size]
+    wanted = laid_out(blocks_2, 0)
     relative = wanted - lax.axis_index("dom") * owned
     inside = jnp.logical_and(relative >= 0, relative < owned).astype(jnp.float32)
     clipped = jnp.clip(relative, 0, owned - 1)

time: 122 us -> 124 us (1.016)
  blocking collectives: 17.9 us -> 7.8 us
  waiting for transfers between devices: 33 us -> 42.7 us
  starting transfers between devices: 18.9 us -> 21.8 us
    all_gather x1 -> x0, blocking collectives: 10.1 us -> none  [on_device(): wanted = lax.all_gather(block_partition, 'dom', axis=0, tiled=True)]
    ppermute x0 -> x3, waiting for transfers between devices: none -> 9.66 us  [the longest x2 9.66 us: on_device(): lax.ppermute(lower_2[-1] if lower_2 else block_partition, 'dom', pairs)]
    ppermute x0 -> x3, starting transfers between devices: none -> 3.02 us  [the longest x1 3.01 us: on_device(): lax.ppermute(upper_2[-1] if upper_2 else block_partition, 'dom', back)]
    gather x3, local copies, waits for them, and re-layouts: 6.02 us -> 8.23 us  [on_device(): send_left = left_vectors[clipped] * inside[:, :, None, None]]
    gather x3, local copies, waits for them, and re-layouts: 7.34 us -> 6.03 us  [on_device(): send_right = right_vectors[clipped] * inside[:, :, None, None]]
    unnamed x18 -> x22, local copies, waits for them, and re-layouts: 5.26 us -> 5.27 us
  transfers between devices with their start and end apart: 3 -> 6, of which waited for: 3 -> 5; matrix products, arithmetic and copies ran while one was open for 2% -> 2% of each run, Pallas kernels for 0% -> 0%
where the time goes in v1:
time: 124 us; the launch traced here: 123 us
  waiting for transfers between devices  42.7 us (34%)
  local copies, waits for them, and re-layouts  29.1 us (23%)
  starting transfers between devices  21.8 us (18%)
  matrix products  13.4 us (11%)
  blocking collectives  7.8 us (6%)
  other arithmetic  7.41 us (6%)
    all_to_all x2, waiting for transfers between devices, copy_for_each(): lax.all_to_all(jnp.broadcast_to(x[None], (count, *x.shape)), axis, 0, 0,...  22 us
    all_to_all x2, starting transfers between devices, copy_for_each(): lax.all_to_all(jnp.broadcast_to(x[None], (count, *x.shape)), axis, 0, 0,...  15.1 us
    all_to_all x1, waiting for transfers between devices, in_one_piece(): lax.all_to_all(both, axis, split_axis=split_dim, concat_axis=concat_dim,...  11 us
    ppermute x2, waiting for transfers between devices, on_device(): lax.ppermute(lower_2[-1] if lower_2 else block_partition, 'dom', pairs)  9.66 us
    gather x3, local copies, waits for them, and re-layouts, on_device(): send_left = left_vectors[clipped] * inside[:, :, None, None]  8.23 us
    all_to_all x1, blocking collectives, sum_at_owner(): parts = lax.all_to_all(cut_along(x, dim, count), axis, 0, 0, tiled=True)  7.8 us
    dot_general x1, matrix products, project(): jnp.einsum('nkj,bjnl->bknl', vec_right, lower, precision=lax.Precision.HI...  6.8 us
    dot_general x1, matrix products, project(): jnp.einsum('binl,nik->bknl', scaled, vec_left, precision=lax.Precision.HI...  6.37 us
  transfers between devices with their start and end apart: 6, of which 5 were waited for; matrix products, arithmetic and copies ran while one was open for 2% of the time, Pallas kernels for 0%

profile of v1, /device:TPU:2, one launch (start us, length us, event | category | flops | bytes accessed | tf_op | source)
XLA Modules:
  0.0 123.2 jit_solution(8612370782264748251)
XLA Ops:
  0.6 0.0 copy-start
  0.6 0.8 copy.100
  1.5 3.0 %collective-permute-start.2 = (s32[1,8]{1,0:T(1,128)}, s32[1,8]{1,0:T(1,128)S(1)}, u32[]{:S(2)}, u32[]{:S(2)}) collective-permute-start(s32[1,8]{1,0:T(1,128)} %param.20), channel_id=1, source_target_pairs={{1,0},{2,1},{3,2},{0,3},{5,4},{6,5},{7,6},{4,7},{9,8},{10,9},{11,1... | collective-permute-start | bytes 104 | tf_op jit(solution)/shard_map/ppermute | solution.py:102
  4.5 0.0 collective-permute-start
  4.5 4.9 %collective-permute-done = s32[1,8]{1,0:T(1,128)S(1)} collective-permute-done((s32[1,8]{1,0:T(1,128)}, s32[1,8]{1,0:T(1,128)S(1)}, u32[]{:S(2)}, u32[]{:S(2)}) %collective-permute-start) | collective-permute-done | bytes 64 | tf_op jit(solution)/shard_map/ppermute | solution.py:100
  9.4 0.0 collective-permute-start.1
  9.4 0.0 collective-permute-done.2
  9.4 4.8 %collective-permute-done.1 = s32[1,8]{1,0:T(1,128)S(1)} collective-permute-done((s32[1,8]{1,0:T(1,128)S(1)}, s32[1,8]{1,0:T(1,128)S(1)}, u32[]{:S(2)}, u32[]{:S(2)}) %collective-permute-start.1) | collective-permute-done | bytes 64 | tf_op jit(solution)/shard_map/ppermute | solution.py:100
  14.2 0.7 pad_add_fusion
  14.9 0.6 gather_fusion
  15.4 0.1 reshape.220
  15.5 0.0 copy-done
  15.5 2.7 %gather_fusion.2 = f32[32,61,61]{2,0,1:T(8,128)S(1)} fusion(f32[64,61,61]{2,0,1:T(8,128)S(1)} %copy-done, s32[1024]{0:T(1024)S(1)} %pad_clamp_fusion.1), kind=kCustom, calls=%fused_computation.2 | custom fusion | bytes 952704 | tf_op jit(solution)/shard_map/gather | solution.py:111
  18.3 1.6 %copy.65 = f32[32,61,61]{2,1,0:T(8,128)} copy(f32[32,61,61]{2,0,1:T(8,128)S(1)} %gather_fusion.2) | data formatting | bytes 952576 | tf_op jit(solution)/shard_map/gather | solution.py:111
  19.9 1.7 %gather.31 = f32[4,8,3721]{2,1,0:T(8,128)S(1)} reshape(f32[32,61,61]{2,1,0:T(8,128)} %copy.65) | data formatting | bytes 952576 | tf_op jit(solution)/shard_map/gather | solution.py:111
  21.6 4.9 %gather_fusion.1 = f32[32,61,61]{2,0,1:T(8,128)S(1)} fusion(f32[64,61,61]{2,0,1:T(8,128)} %param.13, s32[1024]{0:T(1024)S(1)} %pad_clamp_fusion.1), kind=kCustom, calls=%fused_computation.1 | custom fusion | bytes 952704 | tf_op jit(solution)/shard_map/gather | solution.py:110
  26.5 0.0 copy-start.1
  26.5 1.6 %copy.64 = f32[32,61,61]{2,1,0:T(8,128)} copy(f32[32,61,61]{2,0,1:T(8,128)S(1)} %gather_fusion.1) | data formatting | bytes 952576 | tf_op jit(solution)/shard_map/gather | solution.py:110
  28.1 1.7 %gather.29 = f32[4,8,3721]{2,1,0:T(8,128)S(1)} reshape(f32[32,61,61]{2,1,0:T(8,128)} %copy.64) | data formatting | bytes 952576 | tf_op jit(solution)/shard_map/gather | solution.py:110
  29.8 0.6 gather_fusion.4
  30.4 1.3 %gather_fusion.3 = f32[32,61]{1,0:T(8,128)S(1)} fusion(f32[64,61]{1,0:T(8,128)} %param.15, s32[1024]{0:T(1024)S(1)} %pad_clamp_fusion.1), kind=kCustom, calls=%fused_computation.3 | custom fusion | bytes 15744 | tf_op jit(solution)/shard_map/gather | solution.py:112
  31.8 0.1 copy.66
  31.9 0.7 gather_fusion.5
  32.6 0.1 gather.52
  32.7 0.9 broadcast_multiply_fusion
  33.6 0.1 bitcast_multiply_fusion.1
  33.7 2.2 %concatenate.3 = f32[4,8,7565]{2,1,0:T(8,128)} concatenate(f32[4,8,3721]{2,1,0:T(8,128)} %get-tuple-element.29, f32[4,8,3721]{2,1,0:T(8,128)S(1)} %get-tuple-element.28, f32[4,8,61]{2,1,0:T(8,128)S(1)} %get-tuple-element.27, f32[4,8,61]{2,1,0:T(8,128)S(1)} %get-tuple-element.26, f32[4,8,1]{2,1,0:T(8,128)S(1)} %broadcast_select_fusion), dimensions={2} | concatenate | bytes 1936640 | tf_op jit(solution)/shard_map/concatenate | solution.py:18
  35.9 3.7 %all-to-all-start = ((f32[4,8,7565]{2,1,0:T(8,128)}), f32[4,8,7565]{2,1,0:T(8,128)S(1)}, u32[]{:S(2)}, u32[]{:S(2)}) async-start(f32[4,8,7565]{2,1,0:T(8,128)} %concatenate.3), calls=%async_computation | async-start | bytes 1966080 | tf_op jit(solution)/shard_map/all_to_all | solution.py:21
  39.6 0.7 compare_select_fusion.1
  40.3 0.7 gather_fusion.6
  41.0 11.0 %all-to-all-done = f32[4,8,7565]{2,1,0:T(8,128)S(1)} async-done(((f32[4,8,7565]{2,1,0:T(8,128)}), f32[4,8,7565]{2,1,0:T(8,128)S(1)}, u32[]{:S(2)}, u32[]{:S(2)}) %all-to-all-start) | async-done | bytes 968352 | tf_op jit(solution)/shard_map/all_to_all | solution.py:21
  52.0 0.2 slice_reduce_fusion.1
  52.2 0.3 reshape.299
  52.5 1.0 reduce_sum.131
  53.5 0.1 slice_reduce_fusion.4
  53.5 0.2 slice_reduce_fusion.2
  53.7 0.1 multiply_bitcast_fusion
  53.8 0.1 multiply_exponential_fusion
  53.9 0.0 copy-start.7
  53.9 6.8 %fusion = f32[8,61,16,128]{3,1,2,0:T(8,128)S(1)} fusion(f32[16,61,8,128]{3,2,1,0:T(8,128)} %bitcast.46, f32[8,61,61,1]{2,1,0,3:T(8,128)S(1)} %reshape.299), kind=kOutput, calls=%fused_computation.9 | convolution fusion | flops 731578368 | bytes 8114464 | tf_op jit(solution)/shard_map/nkj,bjnl->bknl/dot_general | solution.py:50
  60.7 0.0 copy-start.6
  60.8 6.4 %multiply_reduce_fusion.1 = (f32[16,8,128]{2,0,1:T(8,128)S(1)}, f32[16,8,128]{2,0,1:T(8,128)S(1)}, f32[16,8,128]{2,0,1:T(8,128)S(1)}) fusion(f32[61,8]{0,1:T(8,128)S(1)} %multiply_bitcast_fusion, f32[16,61,8]{1,0,2:T(8,128)S(1)} %multiply_exponential_fusion, f32[8,61,16,128]{3,1,2,0:T(8,128)S(1)} %fusion, f32[16,61,8,128]{3,2,1,0:T(8,128)S(1)} %bitcast.60, ...), kind=kOutput, calls=%fused_computation.14 | convolution fusion | flops 739524608 | bytes 8346208 | tf_op jit(solution)/shard_map/binl,nik->bknl/dot_general | solution.py:49
  67.1 0.1 multiply_reduce_fusion.3
  67.3 0.2 fusion.6
  67.5 0.1 reshape.206
  67.6 0.1 reshape.302
  67.7 7.8 %all_to_all.20 = f32[4,1,2048]{2,1,0:T(1,128)S(1)} all-to-all(f32[4,1,2048]{2,1,0:T(1,128)S(1)} %reshape.302), channel_id=1, replica_groups=mesh['site'=64,'dom'=4] {'dom'}, dimensions={0} | all-to-all | bytes 65536 | tf_op jit(solution)/shard_map/all_to_all | solution.py:34
  75.5 0.5 broadcast.260
  76.0 0.7 reduce.4
  76.8 0.1 reshape.303
  76.9 0.1 broadcast_in_dim.7
  77.0 1.4 %reshape.304 = f32[64,1,2048]{2,1,0:T(1,128)} reshape(f32[64,2,16,64]{3,2,1,0:T(8,128)S(1)} %broadcast_in_dim.7) | data formatting | bytes 1048576
  78.4 11.9 %all-to-all-start.2 = ((f32[64,1,2048]{2,1,0:T(1,128)}), f32[64,1,2048]{2,1,0:T(1,128)S(1)}, u32[]{:S(2)}, u32[]{:S(2)}) async-start(f32[64,1,2048]{2,1,0:T(1,128)} %reshape.304), calls=%async_computation.2 | async-start | bytes 1048576 | tf_op jit(solution)/shard_map/all_to_all | solution.py:40
  90.4 17.5 %all-to-all-done.2 = f32[64,1,2048]{2,1,0:T(1,128)S(1)} async-done(((f32[64,1,2048]{2,1,0:T(1,128)}), f32[64,1,2048]{2,1,0:T(1,128)S(1)}, u32[]{:S(2)}, u32[]{:S(2)}) %all-to-all-start.2) | async-done | bytes 524320 | tf_op jit(solution)/shard_map/all_to_all | solution.py:40
  107.9 2.8 %reduce.5 = f32[64,2048]{1,0:T(8,128)} reduce(f32[64,1,2048]{2,1,0:T(1,128)S(1)} %all-to-all-done.2, f32[]{:T(128)} %broadcast.260), dimensions={1}, to_apply=%all_to_all.14.reduce_sub_computation | reduce | bytes 1048580 | tf_op jit(solution)/shard_map/all_to_all | solution.py:40
  110.7 1.5 %reshape.305 = f32[64,2,16,64]{3,2,1,0:T(8,128)S(1)} reshape(f32[64,2048]{1,0:T(8,128)} %reduce.5) | data formatting | bytes 1048576
  112.1 0.7 fusion.16
  112.8 0.6 broadcast_in_dim.8
  113.4 3.2 %all-to-all-start.3 = ((f32[4,2,16]{2,1,0:T(2,128)}), f32[4,2,16]{2,1,0:T(2,128)S(1)}, u32[]{:S(2)}, u32[]{:S(2)}) async-start(f32[4,2,16]{2,1,0:T(2,128)} %broadcast_in_dim.8), calls=%async_computation.3 | async-start | bytes 8192 | tf_op jit(solution)/shard_map/all_to_all | solution.py:40
  116.7 0.7 copy.78
  117.4 4.5 %all-to-all-done.3 = f32[4,2,16]{2,1,0:T(2,128)S(1)} async-done(((f32[4,2,16]{2,1,0:T(2,128)}), f32[4,2,16]{2,1,0:T(2,128)S(1)}, u32[]{:S(2)}, u32[]{:S(2)}) %all-to-all-start.3) | async-done | bytes 544 | tf_op jit(solution)/shard_map/all_to_all | solution.py:40
  122.0 0.6 scatter_fusion
  122.6 0.0 copy-start.2
  122.6 0.6 copy-done.2
  (24 shorter events, 0.2 us)
Async XLA Ops:
  0.6 14.9 %copy-start = (f32[64,61,61]{2,0,1:T(8,128)S(1)}, f32[64,61,61]{2,0,1:T(8,128)}, u32[]{:S(2)}) copy-start(f32[64,61,61]{2,0,1:T(8,128)} %param.14) | copy-start | bytes 2857732
  1.5 7.9 %collective-permute-start.2 = (s32[1,8]{1,0:T(1,128)}, s32[1,8]{1,0:T(1,128)S(1)}, u32[]{:S(2)}, u32[]{:S(2)}) collective-permute-start(s32[1,8]{1,0:T(1,128)} %param.20), channel_id=1, source_target_pairs={{1,0},{2,1},{3,2},{0,3},{5,4},{6,5},{7,6},{4,7},{9,8},{10,9},{11,1... | collective-permute-start | bytes 104 | tf_op jit(solution)/shard_map/ppermute | solution.py:102
  4.5 4.9 %collective-permute-start = (s32[1,8]{1,0:T(1,128)}, s32[1,8]{1,0:T(1,128)S(1)}, u32[]{:S(2)}, u32[]{:S(2)}) collective-permute-start(s32[1,8]{1,0:T(1,128)} %param.20), channel_id=1, source_target_pairs={{0,1},{1,2},{2,3},{3,0},{4,5},{5,6},{6,7},{7,4},{8,9},{9,10},{10,1... | collective-permute-start | bytes 104 | tf_op jit(solution)/shard_map/ppermute | solution.py:100
  9.4 4.8 %collective-permute-start.1 = (s32[1,8]{1,0:T(1,128)S(1)}, s32[1,8]{1,0:T(1,128)S(1)}, u32[]{:S(2)}, u32[]{:S(2)}) collective-permute-start(s32[1,8]{1,0:T(1,128)S(1)} %collective-permute-done), channel_id=1, source_target_pairs={{0,1},{1,2},{2,3},{3,0},{4,5},{5,6},{6,7},{7,4},{8,9},{9,10},{10,1... | collective-permute-start | bytes 104 | tf_op jit(solution)/shard_map/ppermute | solution.py:100
  21.6 8.3 %copy-start.3 = (f32[64,61]{1,0:T(8,128)S(1)}, f32[64,61]{1,0:T(8,128)}, u32[]{:S(2)}) copy-start(f32[64,61]{1,0:T(8,128)} %param.16) | copy-start | bytes 46852
  26.5 5.4 %copy-start.1 = (f32[64]{0:T(128)S(1)}, f32[64]{0:T(128)}, u32[]{:S(2)}) copy-start(f32[64]{0:T(128)} %param.17) | copy-start | bytes 772
  30.4 9.2 %copy-start.5 = (s32[1,1024]{1,0:T(1,128)S(1)}, s32[1,1024]{1,0:T(1,128)}, u32[]{:S(2)}) copy-start(s32[1,1024]{1,0:T(1,128)} %param.19) | copy-start | bytes 12292
  35.9 16.1 %all-to-all-start = ((f32[4,8,7565]{2,1,0:T(8,128)}), f32[4,8,7565]{2,1,0:T(8,128)S(1)}, u32[]{:S(2)}, u32[]{:S(2)}) async-start(f32[4,8,7565]{2,1,0:T(8,128)} %concatenate.3), calls=%async_computation | async-start | bytes 1966080 | tf_op jit(solution)/shard_map/all_to_all | solution.py:21
  53.9 6.8 %copy-start.4 = (f32[8,61,61]{2,1,0:T(8,128)S(1)}, f32[8,61,61]{2,1,0:T(8,128)}, u32[]{:S(2)}) copy-start(f32[8,61,61]{2,1,0:T(8,128)} %reduce_sum.131) | copy-start | bytes 357220
  53.9 6.8 %copy-start.7 = (f32[16,61,1,1024]{3,2,1,0:T(1,128)S(1)}, f32[16,61,1,1024]{3,2,1,0:T(1,128)}, u32[]{:S(2)}) copy-start(f32[16,61,1,1024]{3,2,1,0:T(1,128)} %param.11) | copy-start | bytes 11993092
  60.7 6.5 %copy-start.6 = (s32[1,8]{1,0:T(1,128)S(1)}, s32[1,8]{1,0:T(1,128)}, u32[]{:S(2)}) copy-start(s32[1,8]{1,0:T(1,128)} %param.20) | copy-start | bytes 100
  78.4 29.4 %all-to-all-start.2 = ((f32[64,1,2048]{2,1,0:T(1,128)}), f32[64,1,2048]{2,1,0:T(1,128)S(1)}, u32[]{:S(2)}, u32[]{:S(2)}) async-start(f32[64,1,2048]{2,1,0:T(1,128)} %reshape.304), calls=%async_computation.2 | async-start | bytes 1048576 | tf_op jit(solution)/shard_map/all_to_all | solution.py:40
  113.4 8.5 %all-to-all-start.3 = ((f32[4,2,16]{2,1,0:T(2,128)}), f32[4,2,16]{2,1,0:T(2,128)S(1)}, u32[]{:S(2)}, u32[]{:S(2)}) async-start(f32[4,2,16]{2,1,0:T(2,128)} %broadcast_in_dim.8), calls=%async_computation.3 | async-start | bytes 8192 | tf_op jit(solution)/shard_map/all_to_all | solution.py:40
  122.6 0.6 copy-start.2
